TPU v7x, 32 devices: a whole 2x2x4 slice. The times are simulated.
32 devices in a mesh: beam: 8 (over y, x, core), tm: 4 (over z).
Axes of the slice: x: 2, y: 2, z: 4, core: 2. Of those that a mesh axis runs over, the one named last changes fastest.
Arguments:
- samples: float32 [2, 18874368], P(None, ('beam', 'tm')), parts along dimension 1, may hold values from -6 to 6
- prototype: float32 [16, 4096], replicated, may hold values from -1.5 to 1.5
Outputs:
- spectra: bfloat16 [2, 6144, 4096], P(None, 'beam', 'tm'), parts along dimension 1
There are 8 independent parts, one for each index of `beam`. A program takes and returns all parts, laid end to end along the dimension named above; an argument that names none is the same for every part. Nothing has to cross between parts.
All inputs are finite; a program needn't handle non-finite values.
Results may differ from a plain program's by a relative error of at most 0.001.
Values may be sent and summed in bfloat16 or wider, within the bound.
A program may use at most 128 MiB of HBM per device.

v0:
```python
import functools
import math

import numpy as np
import jax
import jax.numpy as jnp
from jax import lax
from jax.experimental import pallas as pl
from jax.experimental.pallas import tpu as pltpu
from jax.sharding import PartitionSpec as P

CHANNELS = 4096
TAPS = 16
HOP = 3072
LANES = 128
FIRST = 128
SECOND = CHANNELS // FIRST
ROWS = 2 * CHANNELS // LANES
HOP_ROWS = 2 * HOP // LANES
RIM = TAPS * CHANNELS - HOP
RIM_ROWS = 2 * RIM // LANES
CHUNK = 16
GROUP = 8
MESH = pl.DeviceIdType.MESH


def split_pair(table):
    high = np.asarray(table, np.float32).astype(jnp.bfloat16)
    low = (np.asarray(table, np.float64) - high.astype(np.float64)).astype(jnp.bfloat16)
    return high, low


def first_table():
    b1, a, d = np.meshgrid(np.arange(4), np.arange(32), np.arange(FIRST), indexing="ij")
    angle = 2 * np.pi * ((4 * a + b1) * d % FIRST) / FIRST
    cos, sin = np.cos(angle), np.sin(angle)
    table = np.zeros((4, 32, 2, 2, FIRST))
    table[:, :, 0, 0], table[:, :, 1, 0] = cos, sin
    table[:, :, 0, 1], table[:, :, 1, 1] = -sin, cos
    high, low = split_pair(table.reshape(2 * FIRST, 2 * FIRST))
    return np.concatenate([high, high, low], axis=0)


def middle_table():
    angle = 2 * np.pi * np.outer(np.arange(SECOND), np.arange(FIRST)) / CHANNELS
    return (np.stack([np.cos(angle), np.sin(angle)]) / math.sqrt(CHANNELS)).astype(np.float32)


def second_table():
    angle = 2 * np.pi * (np.outer(np.arange(SECOND), np.arange(SECOND)) % SECOND) / SECOND
    eye = np.eye(GROUP)
    both = np.stack([np.cos(angle), np.sin(angle)])
    table = np.einsum("kcm,tu->kctum", both, eye).reshape(2 * SECOND * GROUP, GROUP * SECOND)
    high, low = split_pair(table)
    return np.concatenate([high, high, low], axis=1)


def split_value(value):
    high = value.astype(jnp.bfloat16)
    low = (value - high.astype(jnp.float32)).astype(jnp.bfloat16)
    return high, low


def partner(me, step, count):
    if count & (count - 1):
        return lax.rem(me + step, count)
    other = me
    bit = 1
    while bit < count:
        if step & bit:
            other = other + bit * (1 - 2 * lax.rem(me // bit, 2))
        bit *= 2
    return other


def kernel(count, frames, x_ref, proto_ref, one_ref, mid_ref, two_ref, out_ref,
           ext, folded, lhs, rhs, staged, load_sem, own_sem, rim_sems, send_sems, recv_sems):
    me = lax.axis_index("tm")
    chunks = frames // CHUNK
    rim_chunks = -(-RIM // (HOP * CHUNK))
    local_rows = frames * HOP_ROWS
    width = CHANNELS // count

    load = pltpu.make_async_copy(x_ref, ext.at[pl.ds(RIM_ROWS, local_rows)], load_sem)
    load.start()

    barrier = pltpu.get_barrier_semaphore()
    for step in range(1, count):
        pl.semaphore_signal(barrier, inc=1, device_id={"tm": partner(me, step, count)}, device_id_type=MESH)
    pl.semaphore_wait(barrier, count - 1)

    def rim_copy():
        return pltpu.make_async_remote_copy(
            src_ref=x_ref.at[pl.ds(local_rows - RIM_ROWS, RIM_ROWS)],
            dst_ref=ext.at[pl.ds(0, RIM_ROWS)],
            send_sem=rim_sems.at[0],
            recv_sem=rim_sems.at[1],
            device_id={"tm": lax.rem(me + 1, count)},
            device_id_type=MESH,
        )

    @pl.when(me < count - 1)
    def _():
        rim_copy().start()

    @pl.when(me == 0)
    def _():
        ext[pl.ds(0, RIM_ROWS), :] = jnp.zeros((RIM_ROWS, LANES), jnp.float32)

    load.wait()
    order = sorted(range(1, count), key=lambda step: (step < count // 2, step))

    def chunk_step(index, carry):
        chunk = lax.rem(index + rim_chunks, chunks)

        @pl.when(jnp.logical_and(index == chunks - rim_chunks, me > 0))
        def _():
            rim_copy().wait_recv()

        base = chunk * (CHUNK * HOP_ROWS)

        def fold(v, carry):
            taps = [proto_ref[tap, pl.ds(pl.multiple_of(v * 8, 8), 8), :] for tap in range(TAPS)]
            for t in range(CHUNK):
                total = None
                for tap in range(TAPS):
                    start = pl.multiple_of(base + (HOP_ROWS * t + ROWS * tap) + v * 8, 8)
                    term = taps[tap] * ext[pl.ds(start, 8), :]
                    total = term if total is None else total + term
                turn = (t + 1) * HOP % CHANNELS * 2 // LANES // 8
                place = lax.rem(v + turn, ROWS // 8)
                folded[t, pl.ds(pl.multiple_of(place * 8, 8), 8), :] = total
            return carry

        lax.fori_loop(0, ROWS // 8, fold, 0)

        lane = lax.broadcasted_iota(jnp.int32, (ROWS, LANES), 1)
        even = lax.rem(lane // SECOND, 2) == 0
        for pair in range(CHUNK // 2):
            one, other = folded[2 * pair], folded[2 * pair + 1]
            upper = jnp.where(even, one, pltpu.roll(other, SECOND, 1))
            lower = jnp.where(even, pltpu.roll(one, LANES - SECOND, 1), other)
            turned = jnp.concatenate([upper, lower], axis=0).T
            high, low = split_value(turned)
            for side in range(2):
                rows = pl.ds((2 * pair + side) * SECOND, SECOND)
                for half in range(2):
                    start = (2 * half + side) * SECOND
                    piece = high[start:start + SECOND]
                    lhs[rows, pl.ds(half * LANES, LANES)] = piece
                    lhs[rows, pl.ds((2 + half) * LANES, LANES)] = low[start:start + SECOND]
                    lhs[rows, pl.ds((4 + half) * LANES, LANES)] = piece

        cos, sin = mid_ref[0], mid_ref[1]
        results = []
        for group in range(CHUNK // GROUP):
            size = GROUP * SECOND
            section = jnp.dot(lhs[pl.ds(group * size, size), :], one_ref[...],
                              preferred_element_type=jnp.float32)
            for t in range(GROUP):
                real = section[t * SECOND:(t + 1) * SECOND, :FIRST]
                imag = section[t * SECOND:(t + 1) * SECOND, FIRST:]
                for half, value in enumerate((real * cos + imag * sin, imag * cos - real * sin)):
                    high, low = split_value(value)
                    columns = pl.ds(half * FIRST, FIRST)
                    rhs[group, pl.ds(t * SECOND, SECOND), columns] = high
                    rhs[group, pl.ds(size + t * SECOND, SECOND), columns] = low
                    rhs[group, pl.ds(2 * size + t * SECOND, SECOND), columns] = high
            product = jnp.dot(two_ref[...], rhs[group], preferred_element_type=jnp.float32)
            results.append((product[:size, :FIRST] + product[size:, FIRST:],
                            product[:size, FIRST:] - product[size:, :FIRST]))
        for part in range(2):
            for c in range(SECOND):
                block = jnp.concatenate(
                    [results[group][part][c * GROUP:(c + 1) * GROUP] for group in range(CHUNK // GROUP)], axis=0)
                owner, at = divmod(c * FIRST, width)
                staged[chunk, owner, part, :, pl.ds(at, FIRST)] = block.astype(jnp.bfloat16)

        rows = pl.ds(pl.multiple_of(me * frames + chunk * CHUNK, CHUNK), CHUNK)
        for step in order:
            to = partner(me, step, count)
            pltpu.make_async_remote_copy(
                src_ref=staged.at[chunk, to],
                dst_ref=out_ref.at[:, rows, :],
                send_sem=send_sems.at[step - 1],
                recv_sem=recv_sems.at[step - 1],
                device_id={"tm": to},
                device_id_type=MESH,
            ).start()
        pltpu.make_async_copy(staged.at[chunk, me], out_ref.at[:, rows, :], own_sem).start()
        return carry

    lax.fori_loop(0, chunks, chunk_step, 0)

    def block_of(device):
        return out_ref.at[:, pl.ds(pl.multiple_of(device * frames, CHUNK), frames), :]

    @pl.when(me < count - 1)
    def _():
        rim_copy().wait_send()

    pltpu.make_async_copy(block_of(me), block_of(me), own_sem).wait()
    for step in order:
        source = partner(me, step, count) if not count & (count - 1) else lax.rem(me + count - step, count)
        whole = pltpu.make_async_remote_copy(
            src_ref=block_of(source),
            dst_ref=block_of(source),
            send_sem=send_sems.at[step - 1],
            recv_sem=recv_sems.at[step - 1],
            device_id={"tm": partner(me, step, count)},
            device_id_type=MESH,
        )
        whole.wait_send()
        whole.wait_recv()


def local(count, samples, prototype):
    frames = samples.shape[1] // HOP
    rows = samples.shape[1] // LANES
    interleaved = samples.reshape(2, rows, LANES).transpose(1, 0, 2).reshape(2 * rows, LANES)
    taps = jnp.repeat(prototype.reshape(TAPS, CHANNELS // LANES, LANES), 2, axis=1)
    vmem = pl.BlockSpec(memory_space=pltpu.VMEM)
    anywhere = pl.BlockSpec(memory_space=pl.ANY)
    width = CHANNELS // count
    return pl.pallas_call(
        functools.partial(kernel, count, frames),
        out_shape=jax.ShapeDtypeStruct((2, frames * count, width), jnp.bfloat16),
        in_specs=[anywhere, vmem, vmem, vmem, vmem],
        out_specs=anywhere,
        scratch_shapes=[
            pltpu.VMEM((RIM_ROWS + 2 * rows, LANES), jnp.float32),
            pltpu.VMEM((CHUNK, ROWS, LANES), jnp.float32),
            pltpu.VMEM((CHUNK * SECOND, 6 * LANES), jnp.bfloat16),
            pltpu.VMEM((CHUNK // GROUP, 3 * GROUP * SECOND, 2 * FIRST), jnp.bfloat16),
            pltpu.VMEM((frames // CHUNK, count, 2, CHUNK, width), jnp.bfloat16),
            pltpu.SemaphoreType.DMA,
            pltpu.SemaphoreType.DMA,
            pltpu.SemaphoreType.DMA((2,)),
            pltpu.SemaphoreType.DMA((count - 1,)),
            pltpu.SemaphoreType.DMA((count - 1,)),
        ],
        compiler_params=pltpu.CompilerParams(
            collective_id=0, has_side_effects=True, vmem_limit_bytes=48 * 1024 * 1024
        ),
    )(interleaved, taps, jnp.asarray(first_table()), jnp.asarray(middle_table()), jnp.asarray(second_table()))


def solution(mesh):
    count = mesh.shape["tm"]
    placed = (P(None, ("beam", "tm")), P())
    return jax.shard_map(
        functools.partial(local, count), mesh=mesh, in_specs=placed,
        out_specs=P(None, "beam", "tm"), check_vma=False,
    )
```

profile of v0, /device:TPU:16, one launch (start us, length us, event | category | flops | bytes accessed | tf_op | source)
XLA Modules:
  0.0 87.6 jit_solution(9625352425546402274)
XLA Ops:
  0.0 1.0 %copy.7 = f32[2,8,32,128]{3,2,1,0:T(8,128)S(1)} copy(f32[2,8,32,128]{3,1,2,0:T(8,128)} %bitcast.11) | data formatting | bytes 524288
  1.0 0.2 broadcast_in_dim.3
  1.2 0.0 copy-start
  1.2 1.1 %copy-done = bf16[512,768]{1,0:T(8,128)(2,1)S(1)} copy-done((bf16[512,768]{1,0:T(8,128)(2,1)S(1)}, bf16[512,768]{1,0:T(8,128)(2,1)}, u32[]{:S(2)}) %copy-start) | copy-done | bytes 786456
  2.3 0.0 copy-start.1
  2.3 1.0 %copy-done.1 = bf16[768,256]{1,0:T(8,128)(2,1)S(1)} copy-done((bf16[768,256]{1,0:T(8,128)(2,1)S(1)}, bf16[768,256]{1,0:T(8,128)(2,1)}, u32[]{:S(2)}) %copy-start.1) | copy-done | bytes 393240
  3.3 0.0 copy-start.2
  3.3 0.8 copy-done.2
  4.1 81.9 %shard_map.55 = bf16[2,768,1024]{2,1,0:T(8,128)(2,1)S(1)} custom-call(f32[9216,128]{1,0:T(8,128)} %bitcast.9, f32[16,64,128]{2,1,0:T(8,128)S(1)} %bitcast.8, bf16[768,256]{1,0:T(8,128)(2,1)S(1)} %copy-done.1, f32[2,32,128]{2,1,0:T(8,128)S(1)} %copy-done.2, bf16[512,768]{1,0:T(8,128)(2,1)S(1)} %copy-done), custom_call_target="tpu_custom_call" | custom-call | tf_op jit(solution)/shard_map/pallas_call | solution.py:225
  86.0 1.7 %copy.9 = bf16[2,768,1024]{2,1,0:T(8,128)(2,1)} copy(bf16[2,768,1024]{2,1,0:T(8,128)(2,1)S(1)} %shard_map.55) | data formatting | bytes 6291456
Async XLA Ops:
  1.2 1.1 %copy-start = (bf16[512,768]{1,0:T(8,128)(2,1)S(1)}, bf16[512,768]{1,0:T(8,128)(2,1)}, u32[]{:S(2)}) copy-start(bf16[512,768]{1,0:T(8,128)(2,1)} %constant.8.clone.two_ref) | copy-start | bytes 2359300
  2.3 1.0 %copy-start.1 = (bf16[768,256]{1,0:T(8,128)(2,1)S(1)}, bf16[768,256]{1,0:T(8,128)(2,1)}, u32[]{:S(2)}) copy-start(bf16[768,256]{1,0:T(8,128)(2,1)} %constant.6.clone.one_ref) | copy-start | bytes 1179652
  3.3 0.8 copy-start.2
where the time goes:
time: 87.9 us; the launch traced here: 87.6 us
  Pallas kernels  81.9 us (93%)
  local copies, waits for them, and re-layouts  5.73 us (7%)
    pallas_call x1, Pallas kernels, local(): pl.pallas_call(functools.partial(kernel, count, frames), out_shape=jax.Sh...  81.9 us
    unnamed x8, local copies, waits for them, and re-layouts  5.55 us

commit v1 on v0

--- a/solution.py
+++ b/solution.py
@@ -73,49 +73,88 @@
     return other
 
 
-def kernel(count, frames, x_ref, proto_ref, one_ref, mid_ref, two_ref, out_ref,
-           ext, folded, lhs, rhs, staged, load_sem, own_sem, rim_sems, send_sems, recv_sems):
+def kernel(count, frames, x_hbm, proto_hbm, one_hbm, mid_hbm, two_hbm, out_ref,
+           ext, raw, spread, proto_ref, one_ref, mid_ref, two_ref, folded, lhs, rhs, staged,
+           load_sems, own_sem, rim_sems, head_sems, send_sems, recv_sems):
     me = lax.axis_index("tm")
     chunks = frames // CHUNK
-    rim_chunks = -(-RIM // (HOP * CHUNK))
     local_rows = frames * HOP_ROWS
+    head_rows = CHUNK * HOP_ROWS
+    past_rows = RIM_ROWS - head_rows
     width = CHANNELS // count
 
-    load = pltpu.make_async_copy(x_ref, ext.at[pl.ds(RIM_ROWS, local_rows)], load_sem)
-    load.start()
+    loads = [
+        pltpu.make_async_copy(source, target, load_sems.at[at])
+        for at, (source, target) in enumerate((
+            (proto_hbm, raw),
+            (x_hbm, ext.at[pl.ds(RIM_ROWS, local_rows)]),
+            (one_hbm, one_ref),
+            (mid_hbm, mid_ref),
+            (two_hbm, two_ref),
+        ))
+    ]
+    for load in loads:
+        load.start()
 
     barrier = pltpu.get_barrier_semaphore()
     for step in range(1, count):
         pl.semaphore_signal(barrier, inc=1, device_id={"tm": partner(me, step, count)}, device_id_type=MESH)
     pl.semaphore_wait(barrier, count - 1)
 
-    def rim_copy():
+    def past_copy():
         return pltpu.make_async_remote_copy(
-            src_ref=x_ref.at[pl.ds(local_rows - RIM_ROWS, RIM_ROWS)],
-            dst_ref=ext.at[pl.ds(0, RIM_ROWS)],
+            src_ref=x_hbm.at[pl.ds(local_rows - past_rows, past_rows)],
+            dst_ref=ext.at[pl.ds(head_rows, past_rows)],
             send_sem=rim_sems.at[0],
             recv_sem=rim_sems.at[1],
             device_id={"tm": lax.rem(me + 1, count)},
             device_id_type=MESH,
         )
 
+    def head_copy():
+        return pltpu.make_async_remote_copy(
+            src_ref=x_hbm.at[pl.ds(0, head_rows)],
+            dst_ref=ext.at[pl.ds(RIM_ROWS + local_rows, head_rows)],
+            send_sem=head_sems.at[0],
+            recv_sem=head_sems.at[1],
+            device_id={"tm": lax.rem(me + count - 1, count)},
+            device_id_type=MESH,
+        )
+
     @pl.when(me < count - 1)
     def _():
-        rim_copy().start()
+        past_copy().start()
+
+    @pl.when(me > 0)
+    def _():
+        head_copy().start()
 
     @pl.when(me == 0)
     def _():
         ext[pl.ds(0, RIM_ROWS), :] = jnp.zeros((RIM_ROWS, LANES), jnp.float32)
 
-    load.wait()
+    loads[0].wait()
+    for row in range(ROWS):
+        spread[pl.ds(row * TAPS, TAPS), :] = raw[:, pl.ds(row // 2 * LANES, LANES)]
+    for tap in range(TAPS):
+        for v in range(ROWS // 8):
+            proto_ref[tap, pl.ds(v * 8, 8), :] = spread[pl.ds(v * 8 * TAPS + tap, 8, stride=TAPS), :]
+    for load in loads[1:]:
+        load.wait()
     order = sorted(range(1, count), key=lambda step: (step < count // 2, step))
 
     def chunk_step(index, carry):
-        chunk = lax.rem(index + rim_chunks, chunks)
-
-        @pl.when(jnp.logical_and(index == chunks - rim_chunks, me > 0))
+        late = chunks - 2
+        chunk = jnp.where(index < late, index + 2,
+                          jnp.where(index == late, 1, jnp.where(index == late + 1, chunks, 0)))
+
+        @pl.when(jnp.logical_and(index == late, me > 0))
         def _():
-            rim_copy().wait_recv()
+            past_copy().wait_recv()
+
+        @pl.when(index == late + 1)
+        def _():
+            head_copy().wait_recv()
 
         base = chunk * (CHUNK * HOP_ROWS)
 
@@ -190,59 +229,78 @@
         pltpu.make_async_copy(staged.at[chunk, me], out_ref.at[:, rows, :], own_sem).start()
         return carry
 
-    lax.fori_loop(0, chunks, chunk_step, 0)
-
-    def block_of(device):
-        return out_ref.at[:, pl.ds(pl.multiple_of(device * frames, CHUNK), frames), :]
+    total = chunks - 1 + jnp.where(me < count - 1, 1, 0) + jnp.where(me == 0, 1, 0)
+    lax.fori_loop(0, total, chunk_step, 0)
 
     @pl.when(me < count - 1)
     def _():
-        rim_copy().wait_send()
-
-    pltpu.make_async_copy(block_of(me), block_of(me), own_sem).wait()
+        past_copy().wait_send()
+
+    @pl.when(me > 0)
+    def _():
+        head_copy().wait_send()
+
+    def each_range(device, act):
+        first, last = device == 0, device == count - 1
+        for chosen, skip, size in (
+            (first, 0, frames + CHUNK),
+            (last, CHUNK, frames - CHUNK),
+            (jnp.logical_not(jnp.logical_or(first, last)), CHUNK, frames),
+        ):
+            @pl.when(chosen)
+            def _():
+                act(out_ref.at[:, pl.ds(pl.multiple_of(device * frames + skip, CHUNK), size), :])
+
+    each_range(me, lambda rows: pltpu.make_async_copy(rows, rows, own_sem).wait())
     for step in order:
-        source = partner(me, step, count) if not count & (count - 1) else lax.rem(me + count - step, count)
-        whole = pltpu.make_async_remote_copy(
-            src_ref=block_of(source),
-            dst_ref=block_of(source),
-            send_sem=send_sems.at[step - 1],
-            recv_sem=recv_sems.at[step - 1],
-            device_id={"tm": partner(me, step, count)},
-            device_id_type=MESH,
-        )
-        whole.wait_send()
-        whole.wait_recv()
+        to = partner(me, step, count)
+        source = to if not count & (count - 1) else lax.rem(me + count - step, count)
+
+        def described(rows):
+            return pltpu.make_async_remote_copy(
+                src_ref=rows, dst_ref=rows, send_sem=send_sems.at[step - 1],
+                recv_sem=recv_sems.at[step - 1], device_id={"tm": to}, device_id_type=MESH)
+
+        each_range(me, lambda rows: described(rows).wait_send())
+        each_range(source, lambda rows: described(rows).wait_recv())
 
 
 def local(count, samples, prototype):
     frames = samples.shape[1] // HOP
     rows = samples.shape[1] // LANES
     interleaved = samples.reshape(2, rows, LANES).transpose(1, 0, 2).reshape(2 * rows, LANES)
-    taps = jnp.repeat(prototype.reshape(TAPS, CHANNELS // LANES, LANES), 2, axis=1)
-    vmem = pl.BlockSpec(memory_space=pltpu.VMEM)
+    one, middle, two = first_table(), middle_table(), second_table()
+    in_hbm = pl.BlockSpec(memory_space=pltpu.HBM)
     anywhere = pl.BlockSpec(memory_space=pl.ANY)
     width = CHANNELS // count
     return pl.pallas_call(
         functools.partial(kernel, count, frames),
         out_shape=jax.ShapeDtypeStruct((2, frames * count, width), jnp.bfloat16),
-        in_specs=[anywhere, vmem, vmem, vmem, vmem],
+        in_specs=[in_hbm] * 5,
         out_specs=anywhere,
         scratch_shapes=[
-            pltpu.VMEM((RIM_ROWS + 2 * rows, LANES), jnp.float32),
+            pltpu.VMEM((RIM_ROWS + 2 * rows + CHUNK * HOP_ROWS, LANES), jnp.float32),
+            pltpu.VMEM(prototype.shape, jnp.float32),
+            pltpu.VMEM((ROWS * TAPS, LANES), jnp.float32),
+            pltpu.VMEM((TAPS, ROWS, LANES), jnp.float32),
+            pltpu.VMEM(one.shape, one.dtype),
+            pltpu.VMEM(middle.shape, middle.dtype),
+            pltpu.VMEM(two.shape, two.dtype),
             pltpu.VMEM((CHUNK, ROWS, LANES), jnp.float32),
             pltpu.VMEM((CHUNK * SECOND, 6 * LANES), jnp.bfloat16),
             pltpu.VMEM((CHUNK // GROUP, 3 * GROUP * SECOND, 2 * FIRST), jnp.bfloat16),
-            pltpu.VMEM((frames // CHUNK, count, 2, CHUNK, width), jnp.bfloat16),
+            pltpu.VMEM((frames // CHUNK + 1, count, 2, CHUNK, width), jnp.bfloat16),
+            pltpu.SemaphoreType.DMA((5,)),
             pltpu.SemaphoreType.DMA,
-            pltpu.SemaphoreType.DMA,
+            pltpu.SemaphoreType.DMA((2,)),
             pltpu.SemaphoreType.DMA((2,)),
             pltpu.SemaphoreType.DMA((count - 1,)),
             pltpu.SemaphoreType.DMA((count - 1,)),
         ],
         compiler_params=pltpu.CompilerParams(
-            collective_id=0, has_side_effects=True, vmem_limit_bytes=48 * 1024 * 1024
+            collective_id=0, has_side_effects=True, vmem_limit_bytes=60300000
         ),
-    )(interleaved, taps, jnp.asarray(first_table()), jnp.asarray(middle_table()), jnp.asarray(second_table()))
+    )(interleaved, prototype, jnp.asarray(one), jnp.asarray(middle), jnp.asarray(two))
 
 
 def solution(mesh):

time: 87.9 us -> 82.8 us (0.942)
  the two profiles are of different devices: /device:TPU:16 before, /device:TPU:0 now
where the time goes in v1:
time: 82.8 us; the launch traced here: 82.7 us
  Pallas kernels  78.8 us (95%)
  local copies, waits for them, and re-layouts  3.86 us (5%)
    pallas_call x1, Pallas kernels, local(): pl.pallas_call(functools.partial(kernel, count, frames), out_shape=jax.Sh...  78.8 us
    unnamed x1, local copies, waits for them, and re-layouts  3.86 us

profile of v1, /device:TPU:0, one launch (start us, length us, event | category | flops | bytes accessed | tf_op | source)
XLA Modules:
  0.0 82.7 jit_solution(12422473764402774730)
XLA Ops:
  0.0 78.8 %shard_map.55 = bf16[2,768,1024]{2,1,0:T(8,128)(2,1)} custom-call(f32[9216,128]{1,0:T(8,128)} %bitcast.5, f32[16,4096]{1,0:T(8,128)} %proto_hbm.1, bf16[768,256]{1,0:T(8,128)(2,1)} %constant.6.clone.one_hbm, f32[2,32,128]{2,1,0:T(8,128)} %constant.7.clone.mid_hbm, bf16[512,768]{1,0:T(8,128)(2,1)} %constant.8.clone.two_hbm), custom_call_target="tpu_custom_call" | custom-call | tf_op jit(solution)/shard_map/pallas_call | solution.py:276
  78.8 3.9 %copy.8 = bf16[2,768,1024]{2,1,0:T(8,128)(2,1)} copy(bf16[2,768,1024]{2,1,0:T(8,128)(2,1)} %shard_map.55) | data formatting | bytes 6291456

commit v2 on v1

--- a/solution.py
+++ b/solution.py
@@ -275,7 +275,7 @@
     width = CHANNELS // count
     return pl.pallas_call(
         functools.partial(kernel, count, frames),
-        out_shape=jax.ShapeDtypeStruct((2, frames * count, width), jnp.bfloat16),
+        out_shape=pltpu.VMEM((2, frames * count, width), jnp.bfloat16),
         in_specs=[in_hbm] * 5,
         out_specs=anywhere,
         scratch_shapes=[

time: 82.8 us -> 80.5 us (0.972)
  local copies, waits for them, and re-layouts: 3.86 us -> 1.67 us
    unnamed x1, local copies, waits for them, and re-layouts: 3.86 us -> 1.67 us
where the time goes in v2:
time: 80.5 us; the launch traced here: 80.4 us
  Pallas kernels  78.7 us (98%)
  local copies, waits for them, and re-layouts  1.67 us (2%)
    pallas_call x1, Pallas kernels, local(): pl.pallas_call(functools.partial(kernel, count, frames), out_shape=pltpu....  78.7 us
    unnamed x1, local copies, waits for them, and re-layouts  1.67 us

profile of v2, /device:TPU:0, one launch (start us, length us, event | category | flops | bytes accessed | tf_op | source)
XLA Modules:
  0.0 80.4 jit_solution(10437727003304071385)
XLA Ops:
  0.0 78.7 %shard_map.55 = bf16[2,768,1024]{2,1,0:T(8,128)(2,1)S(1)} custom-call(f32[9216,128]{1,0:T(8,128)} %bitcast.5, f32[16,4096]{1,0:T(8,128)} %proto_hbm.1, bf16[768,256]{1,0:T(8,128)(2,1)} %constant.6.clone.one_hbm, f32[2,32,128]{2,1,0:T(8,128)} %constant.7.clone.mid_hbm, bf16[512,768]{1,0:T(8,128)(2,1)} %constant.8.clone.two_hbm), custom_call_target="tpu_custom_call" | custom-call | tf_op jit(solution)/shard_map/pallas_call | solution.py:276
  78.7 1.7 %copy.8 = bf16[2,768,1024]{2,1,0:T(8,128)(2,1)} copy(bf16[2,768,1024]{2,1,0:T(8,128)(2,1)S(1)} %shard_map.55) | data formatting | bytes 6291456
